TPU v7x, 32 devices: a whole 2x2x4 slice. The times are simulated.
32 devices in a mesh: grp: 4 (over y, core), blk: 8 (over z, x).
Axes of the slice: x: 2, y: 2, z: 4, core: 2. Of those that a mesh axis runs over, the one named last changes fastest.
Arguments:
- embeds: bfloat16 [4, 8192, 1024], P('grp', 'blk')
- doc_ids: int32 [4, 8192], P('grp', 'blk'), may hold values from 0 to 8191, each once within a row
- prior_max: float32 [4, 8192], P('grp', 'blk'), may hold values from -0.2 to 0.6
- owned: bfloat16 [2048, 1024], P(('grp', 'blk')), may hold values from -6 to 6
- owned_ids: int32 [2048], P(('grp', 'blk')), may hold values from 0 to 2047, each once
- owner_dest: int32 [2048, 1], P(('grp', 'blk')), may hold values from 0 to 31; in each aligned block of 64 rows (0 to 63, 64 to 127, ...) at most 4 rows name the same one
Outputs:
- running_max: float32 [4, 8192], P('grp', 'blk')
- next_rows: bfloat16 [4096, 1024], P(('grp', 'blk'))
- next_ids: int32 [4096], P(('grp', 'blk'))
Inputs may be any that keep to these rules, and one draw needn't show every extreme that they name: `owner_dest`: among the 64 rows of one device no target is named more than 4 times, a bound that some block reaches.
All inputs are finite; a program needn't handle non-finite values.
Results may differ from a plain program's by a relative error of at most 0.0016.
Values may be sent and summed in bfloat16 or wider, within the bound.
A program may use at most 64 MiB of HBM per device.

v0:
```python
import jax
import jax.numpy as jnp
from jax import lax
from jax.sharding import PartitionSpec as P

CYCLE = 3
CAP = 4


def passed_along(value, axis, steps):
    count = lax.axis_size(axis)
    pairs = [(source, (source + steps) % count) for source in range(count)]
    return lax.ppermute(value, axis, pairs)


def normalize(matrix):
    values = matrix.astype(jnp.float32)
    scale = lax.rsqrt(jnp.sum(values * values, axis=-1, keepdims=True) + 1e-06)
    return (values * scale).astype(jnp.bfloat16)


def tile_max(row_normed, row_ids, col_normed, col_ids):
    scores = lax.dot_general(
        row_normed, col_normed, (((1,), (1,)), ((), ())), preferred_element_type=jnp.float32
    )
    masked = jnp.where(col_ids[None, :] < row_ids[:, None], scores, jnp.float32(-2.0))
    return jnp.max(masked, axis=1)


def body(embeds, doc_ids, prior_max, owned, owned_ids, owner_dest):
    devices = lax.axis_size("grp") * lax.axis_size("blk")
    owned_normed = normalize(owned)
    target = owner_dest[:, 0]
    onehot = (target[:, None] == jnp.arange(devices, dtype=jnp.int32)[None, :]).astype(jnp.int32)
    position = jnp.sum(jnp.cumsum(onehot, axis=0) * onehot, axis=1) - 1
    place = target * CAP + position
    width = owned.shape[1]
    outgoing = jnp.zeros((devices * CAP, width), jnp.bfloat16).at[place].set(owned_normed)
    outgoing_ids = jnp.full((devices * CAP,), -1, jnp.int32).at[place].set(owned_ids)
    arrived, arrived_ids = (
        lax.all_to_all(
            outgoing.reshape(devices, CAP, width),
            ("grp", "blk"),
            split_axis=0,
            concat_axis=0,
            tiled=True,
        ),
        lax.all_to_all(
            outgoing_ids.reshape(devices, CAP),
            ("grp", "blk"),
            split_axis=0,
            concat_axis=0,
            tiled=True,
        ),
    )
    next_rows = arrived.reshape(devices * CAP, width)
    next_ids = arrived_ids.reshape(devices * CAP)
    normed = normalize(embeds[0])
    numbers = doc_ids[0]
    running = jnp.maximum(prior_max[0], tile_max(normed, numbers, normed, numbers))
    carried = (normed, numbers)
    for stride in range(CYCLE):
        carried = passed_along((carried[0], carried[1]), "blk", 1)
        running = jnp.maximum(running, tile_max(normed, numbers, carried[0], carried[1]))
    return (running[None, :], next_rows, next_ids)


def solution(mesh):
    return jax.shard_map(
        body,
        mesh=mesh,
        in_specs=(
            P("grp", "blk", None),
            P("grp", "blk"),
            P("grp", "blk"),
            P(("grp", "blk"), None),
            P(("grp", "blk")),
            P(("grp", "blk"), None),
        ),
        out_specs=(P("grp", "blk"), P(("grp", "blk"), None), P(("grp", "blk"))),
        check_vma=False,
    )
```

profile of v0, /device:TPU:0, one launch (start us, length us, event | category | flops | bytes accessed | tf_op | source)
XLA Modules:
  0.0 183.6 jit_solution(3679627430762162577)
XLA Ops:
  0.6 2.2 %fusion.2 = f32[1024]{0:T(1024)S(1)} fusion(bf16[1,1024,1024]{2,1,0:T(8,128)(2,1)} %param.6), kind=kLoop, calls=%fused_computation.6 | loop fusion | flops 3144704 | bytes 2101248 | tf_op jit(solution)/shard_map/reduce_sum | solution.py:18
  3.3 1.3 copy-done.1
  4.7 3.0 %collective-permute-start.1 = (bf16[1024,1024]{1,0:T(8,128)(2,1)S(1)}, bf16[1024,1024]{1,0:T(8,128)(2,1)}, u32[]{:S(2)}, u32[]{:S(2)}) collective-permute-start(bf16[1024,1024]{1,0:T(8,128)(2,1)S(1)} %fusion.3), channel_id=1, source_target_pairs={{0,1},{1,2},{2,3},{3,4},{4,5},{5,6},{6,7},{7,0},{8,9},{9,10},{10,1... | collective-permute-start | bytes 6291464 | tf_op jit(solution)/shard_map/ppermute | solution.py:13
  7.6 48.8 %collective-permute-done.1 = bf16[1024,1024]{1,0:T(8,128)(2,1)} collective-permute-done((bf16[1024,1024]{1,0:T(8,128)(2,1)S(1)}, bf16[1024,1024]{1,0:T(8,128)(2,1)}, u32[]{:S(2)}, u32[]{:S(2)}) %collective-permute-start.1) | collective-permute-done | bytes 2097184 | tf_op jit(solution)/shard_map/ppermute | solution.py:13
  56.4 1.1 collective-permute-start
  57.9 48.3 %collective-permute-done.3 = bf16[1024,1024]{1,0:T(8,128)(2,1)} collective-permute-done((bf16[1024,1024]{1,0:T(8,128)(2,1)}, bf16[1024,1024]{1,0:T(8,128)(2,1)}, u32[]{:S(2)}, u32[]{:S(2)}) %collective-permute-start.3) | collective-permute-done | bytes 2097184 | tf_op jit(solution)/shard_map/ppermute | solution.py:13
  106.3 0.9 scatter_custom_fusion.1
  107.2 0.7 all_to_all.10
  107.9 5.8 %all-to-all-start.1 = ((s32[32,1,4]{2,1,0:T(1,128)}), s32[32,1,4]{2,1,0:T(1,128)S(1)}, u32[]{:S(2)}, u32[]{:S(2)}) async-start(s32[32,1,4]{2,1,0:T(1,128)} %bitcast.10), calls=%async_computation.1 | async-start | bytes 32768 | tf_op jit(solution)/shard_map/all_to_all | solution.py:48
  113.9 1.0 scatter_custom_fusion
  114.9 0.8 reshape.67
  115.7 1.8 collective-permute-start.2
  117.5 38.5 %all-to-all-done.1 = s32[32,1,4]{2,1,0:T(1,128)S(1)} async-done(((s32[32,1,4]{2,1,0:T(1,128)}), s32[32,1,4]{2,1,0:T(1,128)S(1)}, u32[]{:S(2)}, u32[]{:S(2)}) %all-to-all-start.1) | async-done | bytes 544 | tf_op jit(solution)/shard_map/all_to_all | solution.py:48
  156.0 2.6 %all-to-all-start = ((bf16[32,4,1024]{2,1,0:T(4,128)(2,1)}), bf16[32,4,1024]{2,1,0:T(4,128)(2,1)S(1)}, u32[]{:S(2)}, u32[]{:S(2)}) async-start(bf16[32,4,1024]{2,1,0:T(4,128)(2,1)} %reshape.67), calls=%async_computation | async-start | bytes 524288 | tf_op jit(solution)/shard_map/all_to_all | solution.py:41
  158.6 2.5 %select_reduce_fusion.3 = f32[1024]{0:T(1024)S(1)} fusion(s32[1024]{0:T(1024)S(1)} %bitcast.41, bf16[1,1024,1024]{2,1,0:T(8,128)(2,1)S(1)} %copy-done, f32[1024]{0:T(1024)S(1)} %add_rsqrt_fusion), kind=kOutput, calls=%fused_computation.12 | convolution fusion | flops 2153774080 | bytes 2109440 | tf_op jit(solution)/shard_map/dot_general | solution.py:23
  161.6 0.7 reduce.3
  162.3 0.6 reshape.69
  162.9 1.6 collective-permute-start.4
  164.5 4.5 %all-to-all-done = bf16[32,4,1024]{2,1,0:T(4,128)(2,1)S(1)} async-done(((bf16[32,4,1024]{2,1,0:T(4,128)(2,1)}), bf16[32,4,1024]{2,1,0:T(4,128)(2,1)S(1)}, u32[]{:S(2)}, u32[]{:S(2)}) %all-to-all-start) | async-done | bytes 262176 | tf_op jit(solution)/shard_map/all_to_all | solution.py:41
  169.0 0.8 reshape.68
  169.8 4.7 %fusion.21 = f32[1024,1024]{0,1:T(8,128)S(1)} fusion(bf16[1024,1024]{1,0:T(8,128)(2,1)} %copy-done.1, bf16[1024,1024]{1,0:T(8,128)(2,1)} %collective-permute-done.1), kind=kOutput, calls=%fused_computation.34 | convolution fusion | flops 2147483648 | bytes 8388608 | tf_op jit(solution)/shard_map/dot_general | solution.py:23
  174.5 4.0 %fusion.22 = f32[1024,1024]{0,1:T(8,128)S(1)} fusion(bf16[1024,1024]{1,0:T(8,128)(2,1)S(1)} %copy-done.2, bf16[1024,1024]{1,0:T(8,128)(2,1)} %collective-permute-done.3), kind=kOutput, calls=%fused_computation.35 | convolution fusion | flops 2147483648 | bytes 8388608 | tf_op jit(solution)/shard_map/dot_general | solution.py:23
  178.5 4.5 %select_reduce_fusion.2 = (f32[1024]{0:T(1024)S(1)}, f32[1024]{0:T(1024)S(1)}, f32[1024]{0:T(1024)S(1)}) fusion(f32[1024,1024]{0,1:T(8,128)S(1)} %fusion.21, s32[1024]{0:T(1024)S(1)} %bitcast.42, s32[1024]{0:T(1024)S(1)} %collective-permute-done, f32[1024,1024]{0,1:T(8,128)S(1)} %fusion.22, s32[1024]{0:T(1024)S(1)} %collective-permute-done.2, ...), kind=kOutput, calls=%fused_computation.11 | convolution fusion | flops 2156917760 | bytes 12611584 | tf_op jit(solution)/shard_map/dot_general | solution.py:23
  183.0 0.6 maximum_maximum_fusion
  (28 shorter events, 1.5 us)
Async XLA Ops:
  0.6 2.2 %copy-start = (bf16[1,1024,1024]{2,1,0:T(8,128)(2,1)S(1)}, bf16[1,1024,1024]{2,1,0:T(8,128)(2,1)}, u32[]{:S(2)}) copy-start(bf16[1,1024,1024]{2,1,0:T(8,128)(2,1)} %param.6) | copy-start | bytes 6291460
  2.9 53.5 %copy-start.6 = (s32[1,1024]{1,0:T(1,128)S(1)}, s32[1,1024]{1,0:T(1,128)}, u32[]{:S(2)}) copy-start(s32[1,1024]{1,0:T(1,128)} %param.7) | copy-start | bytes 12292
  2.9 54.7 %copy-start.5 = (s32[64,1]{0,1:T(1,128)S(1)}, s32[64,1]{0,1:T(1,128)}, u32[]{:S(2)}) copy-start(s32[64,1]{0,1:T(1,128)} %param.11) | copy-start | bytes 772
  2.9 110.8 %copy-start.3 = (bf16[64,1024]{1,0:T(8,128)(2,1)S(1)}, bf16[64,1024]{1,0:T(8,128)(2,1)}, u32[]{:S(2)}) copy-start(bf16[64,1024]{1,0:T(8,128)(2,1)} %param.9) | copy-start | bytes 393220
  3.3 1.4 copy-start.1
  4.7 51.7 %collective-permute-start.1 = (bf16[1024,1024]{1,0:T(8,128)(2,1)S(1)}, bf16[1024,1024]{1,0:T(8,128)(2,1)}, u32[]{:S(2)}, u32[]{:S(2)}) collective-permute-start(bf16[1024,1024]{1,0:T(8,128)(2,1)S(1)} %fusion.3), channel_id=1, source_target_pairs={{0,1},{1,2},{2,3},{3,4},{4,5},{5,6},{6,7},{7,0},{8,9},{9,10},{10,1... | collective-permute-start | bytes 6291464 | tf_op jit(solution)/shard_map/ppermute | solution.py:13
  56.4 49.9 %collective-permute-start.3 = (bf16[1024,1024]{1,0:T(8,128)(2,1)}, bf16[1024,1024]{1,0:T(8,128)(2,1)}, u32[]{:S(2)}, u32[]{:S(2)}) collective-permute-start(bf16[1024,1024]{1,0:T(8,128)(2,1)} %collective-permute-done.1), channel_id=1, source_target_pairs={{0,1},{1,2},{2,3},{3,4},{4,5},{5,6},{6,7},{7,0},{8,9},{9,10},{10,1... | collective-permute-start | bytes 6291464 | tf_op jit(solution)/shard_map/ppermute | solution.py:13
  56.4 59.3 %collective-permute-start = (s32[1024]{0:T(1024)S(1)}, s32[1024]{0:T(1024)S(1)}, u32[]{:S(2)}, u32[]{:S(2)}) collective-permute-start(s32[1024]{0:T(1024)S(1)} %bitcast.40), channel_id=1, source_target_pairs={{0,1},{1,2},{2,3},{3,4},{4,5},{5,6},{6,7},{7,0},{8,9},{9,10},{10,1... | collective-permute-start | bytes 12296 | tf_op jit(solution)/shard_map/ppermute | solution.py:13
  106.3 72.3 %collective-permute-start.5 = (bf16[1024,1024]{1,0:T(8,128)(2,1)}, bf16[1024,1024]{1,0:T(8,128)(2,1)}, u32[]{:S(2)}, u32[]{:S(2)}) collective-permute-start(bf16[1024,1024]{1,0:T(8,128)(2,1)} %collective-permute-done.3), channel_id=1, source_target_pairs={{0,1},{1,2},{2,3},{3,4},{4,5},{5,6},{6,7},{7,0},{8,9},{9,10},{10,1... | collective-permute-start | bytes 6291464 | tf_op jit(solution)/shard_map/ppermute | solution.py:13
  107.9 48.1 %all-to-all-start.1 = ((s32[32,1,4]{2,1,0:T(1,128)}), s32[32,1,4]{2,1,0:T(1,128)S(1)}, u32[]{:S(2)}, u32[]{:S(2)}) async-start(s32[32,1,4]{2,1,0:T(1,128)} %bitcast.10), calls=%async_computation.1 | async-start | bytes 32768 | tf_op jit(solution)/shard_map/all_to_all | solution.py:48
  115.7 47.2 %collective-permute-start.2 = (s32[1024]{0:T(1024)S(1)}, s32[1024]{0:T(1024)S(1)}, u32[]{:S(2)}, u32[]{:S(2)}) collective-permute-start(s32[1024]{0:T(1024)S(1)} %collective-permute-done), channel_id=1, source_target_pairs={{0,1},{1,2},{2,3},{3,4},{4,5},{5,6},{6,7},{7,0},{8,9},{9,10},{10,1... | collective-permute-start | bytes 12296 | tf_op jit(solution)/shard_map/ppermute | solution.py:13
  156.0 13.0 %all-to-all-start = ((bf16[32,4,1024]{2,1,0:T(4,128)(2,1)}), bf16[32,4,1024]{2,1,0:T(4,128)(2,1)S(1)}, u32[]{:S(2)}, u32[]{:S(2)}) async-start(bf16[32,4,1024]{2,1,0:T(4,128)(2,1)} %reshape.67), calls=%async_computation | async-start | bytes 524288 | tf_op jit(solution)/shard_map/all_to_all | solution.py:41
  162.9 15.6 %collective-permute-start.4 = (s32[1024]{0:T(1024)S(1)}, s32[1024]{0:T(1024)S(1)}, u32[]{:S(2)}, u32[]{:S(2)}) collective-permute-start(s32[1024]{0:T(1024)S(1)} %collective-permute-done.2), channel_id=1, source_target_pairs={{0,1},{1,2},{2,3},{3,4},{4,5},{5,6},{6,7},{7,0},{8,9},{9,10},{10,1... | collective-permute-start | bytes 12296 | tf_op jit(solution)/shard_map/ppermute | solution.py:13
  169.8 4.8 %copy-start.2 = (bf16[1024,1024]{1,0:T(8,128)(2,1)S(1)}, bf16[1024,1024]{1,0:T(8,128)(2,1)}, u32[]{:S(2)}) copy-start(bf16[1024,1024]{1,0:T(8,128)(2,1)} %copy-done.1) | copy-start | bytes 6291460
  178.5 4.5 %copy-start.4 = (f32[1,1024]{1,0:T(1,128)S(1)}, f32[1,1024]{1,0:T(1,128)}, u32[]{:S(2)}) copy-start(f32[1,1024]{1,0:T(1,128)} %param.8) | copy-start | bytes 12292
where the time goes:
time: 184 us
  waiting for transfers between devices  140 us (76%)
  starting transfers between devices  16 us (9%)
  matrix products  15.6 us (8%)
  local copies, waits for them, and re-layouts  5.69 us (3%)
  other arithmetic  5.43 us (3%)
    ppermute x6, waiting for transfers between devices, passed_along(): return lax.ppermute(value, axis, pairs)  97.1 us
    all_to_all x1, waiting for transfers between devices, body(): lax.all_to_all(outgoing_ids.reshape(devices, CAP), ('grp', 'blk'), split_...  38.5 us
    dot_general x4, matrix products, tile_max(): lax.dot_general(row_normed, col_normed, (((1,), (1,)), ((), ())), preferr...  15.6 us
    ppermute x6, starting transfers between devices, passed_along(): return lax.ppermute(value, axis, pairs)  7.52 us
    all_to_all x1, starting transfers between devices, body(): lax.all_to_all(outgoing_ids.reshape(devices, CAP), ('grp', 'blk'), split_...  5.85 us
    all_to_all x1, waiting for transfers between devices, body(): lax.all_to_all(outgoing.reshape(devices, CAP, width), ('grp', 'blk'), spl...  4.49 us
  transfers between devices with their start and end apart: 8, of which 4 were waited for; matrix products, arithmetic and copies ran while one was open for 9% of the time, Pallas kernels for 0%

commit v1 on v0

v1 whole, which is shorter than its diff:
```python
import functools

import jax
import jax.numpy as jnp
from jax import lax
from jax.experimental import pallas as pl
from jax.experimental.pallas import tpu as pltpu
from jax.sharding import PartitionSpec as P

CYCLE = 3
CAP = 4
CHUNKS = 4
LANES = 128
EMPTY = -2.0


def make_plan(nz):
    if nz == 4:
        received = [[], [(0, 0)], [(1, 1), (0, 1), (3, 3)], [(1, 2), (0, 2)]]
        late = [z == 3 for z in range(nz)]
    else:
        received = [[((z - 1) % nz, (z - 1) % nz), ((z - 2) % nz, (z - 1) % nz)] for z in range(nz)]
        late = [False] * nz
    own_to = [(-1, 0)] * nz
    forward = [[(-1, 0)] * len(received[z]) for z in range(nz)]
    rank = [[0] * len(received[z]) for z in range(nz)]
    returns = [0] * nz
    for z in range(nz):
        for slot, (block, source) in enumerate(received[z]):
            if block == source:
                own_to[source] = (z, slot)
            else:
                held = [entry[0] for entry in received[source]].index(block)
                forward[source][held] = (z, slot)
            rank[z][slot] = returns[block]
            returns[block] += 1
    return received, own_to, late, forward, rank, returns


def pick(index, values):
    result = jnp.int32(values[0])
    for i in range(1, len(values)):
        if values[i] != values[0]:
            result = jnp.where(index == i, jnp.int32(values[i]), result)
    return result


def kernel(plan, sizes, emb, ids, prior, owned, owned_ids, dest,
           run_out, rows_out, ids_out,
           raw, nrm, idv, idt, acc, ret, obuf, oid,
           local_sem, send_sem, recv_sem, ids_send, ids_recv, ret_send, ret_recv,
           rows_send, rows_recv, oids_send, oids_recv, keep_sem):
    n_grp, n_blk = sizes
    devices = n_grp * n_blk
    nz = n_blk // 2
    received, own_to, late, forward, rank, returns = plan
    slots = max(len(entry) for entry in received)
    rows = emb.shape[1]
    ch = rows // CHUNKS
    g = lax.axis_index("grp")
    b = lax.axis_index("blk")
    flip = g % 2
    z = b // 2
    x = b % 2
    role = z + flip * (nz - 1 - 2 * z)

    def block_of(zr):
        return 2 * (zr + flip * (nz - 1 - 2 * zr)) + x

    partner = b + 1 - 2 * x

    def table(values, slot=None, empty=0):
        if slot is None:
            return pick(role, values)
        return pick(role, [v[slot] if slot < len(v) else empty for v in values])

    own_z, own_slot = table([v[0] for v in own_to]), table([v[1] for v in own_to])
    is_late = table([int(v) for v in late])
    exists = [table([[1] * len(v) for v in received], s) for s in range(slots)]
    slot_z = [table([[e[0] for e in v] for v in received], s) for s in range(slots)]
    fwd_z = [table([[e[0] for e in v] for v in forward], s, -1) for s in range(slots)]
    fwd_slot = [table([[e[1] for e in v] for v in forward], s) for s in range(slots)]
    ranks = [table(rank, s) for s in range(slots)]
    n_returns = table(returns)
    blocks = [b, partner] + [block_of(slot_z[s]) for s in range(slots)]

    def span(c):
        if isinstance(c, int):
            return pl.ds(c * ch, ch)
        return pl.ds(pl.multiple_of(c * ch, ch), ch)

    def remote(src, dst, ssem, rsem, blk, grp=None):
        return pltpu.make_async_remote_copy(
            src_ref=src, dst_ref=dst, send_sem=ssem, recv_sem=rsem,
            device_id=(g if grp is None else grp, blk), device_id_type=pl.DeviceIdType.MESH)

    def chunk_copy(src, lane, to_slot, blk, c):
        return remote(src, raw.at[to_slot, span(c), :], send_sem.at[lane, c], recv_sem.at[to_slot, c], blk)

    def ids_copy(src, lane, to_slot, blk):
        return remote(src, idv.at[to_slot], ids_send.at[lane], ids_recv.at[to_slot], blk)

    def own_column(c):
        return chunk_copy(emb.at[0, span(c), :], 1, 2 + own_slot, block_of(own_z), c)

    def partner_copy(c):
        return chunk_copy(emb.at[0, span(c), :], 0, 1, partner, c)

    def forward_copy(s, c):
        return chunk_copy(raw.at[2 + s, span(c), :], 2 + s, 2 + fwd_slot[s], block_of(fwd_z[s]), c)

    def start_own_column():
        ids_copy(ids, 1, 2 + own_slot, block_of(own_z)).start()
        for c in range(CHUNKS):
            own_column(c).start()

    local = pltpu.make_async_copy(emb.at[0], raw.at[0], local_sem)
    local.start()

    @pl.when((own_z >= 0) & (is_late == 0))
    def _():
        start_own_column()

    ids_copy(ids, 0, 1, partner).start()
    for c in range(CHUNKS):
        partner_copy(c).start()

    def normalize(values):
        values = values.astype(jnp.float32)
        scale = lax.rsqrt(jnp.sum(values * values, axis=-1, keepdims=True) + 1e-06)
        return (values * scale).astype(jnp.bfloat16)

    own_dev = owned.shape[0]
    owned_normed = normalize(owned[...])
    t_col = dest[...].astype(jnp.float32)
    t_row = jnp.transpose(jnp.broadcast_to(t_col, (own_dev, LANES)))[0:1, :]
    row_i = lax.broadcasted_iota(jnp.int32, (own_dev, own_dev), 0)
    col_i = lax.broadcasted_iota(jnp.int32, (own_dev, own_dev), 1)
    earlier = jnp.where((row_i < col_i) & (t_col == t_row), 1.0, 0.0)
    position = jnp.sum(earlier, axis=0, keepdims=True)
    place = t_row * CAP + position
    which = lax.broadcasted_iota(jnp.int32, (devices * CAP, own_dev), 0).astype(jnp.float32)
    onehot = jnp.where(which == place, 1.0, 0.0).astype(jnp.bfloat16)
    outgoing = jnp.dot(onehot, owned_normed, preferred_element_type=jnp.float32).astype(jnp.bfloat16)
    dev_i = lax.broadcasted_iota(jnp.int32, (devices, own_dev), 0).astype(jnp.float32)
    lane_i = lax.broadcasted_iota(jnp.int32, (devices, LANES), 1)
    number = owned_ids[...].astype(jnp.float32) + 1.0
    outgoing_ids = jnp.full((devices, LANES), -1.0, jnp.float32)
    for k in range(CAP):
        here = jnp.where((dev_i == t_row) & (position == float(k)), number, 0.0)
        found = jnp.sum(here, axis=1, keepdims=True) - 1.0
        outgoing_ids = jnp.where(lane_i == k, found, outgoing_ids)
    outgoing_ids = outgoing_ids.astype(jnp.int32)
    for d in range(devices):
        obuf[d] = outgoing[d * CAP:(d + 1) * CAP, :]
        oid[d] = outgoing_ids[d:d + 1, :]

    def ready(s, c):
        at = span(c)
        nrm[s, at, :] = normalize(raw[s, at, :])
        for p in range(ch // LANES):
            at = pl.ds(pl.multiple_of(c * ch + p * LANES, LANES), LANES)
            line = idv[s, :, at].astype(jnp.float32)
            idt[s, at, :] = jnp.transpose(jnp.broadcast_to(line, (LANES, LANES)))

    def tile(row, row_at, width, col, col_at):
        scores = lax.dot_general(
            nrm[col, col_at, :], nrm[row, row_at, :], (((1,), (1,)), ((), ())),
            preferred_element_type=jnp.float32)
        row_ids = idv[row, :, row_at].astype(jnp.float32)
        col_ids = idt[col, col_at, :]
        parts = []
        for p in range(width // LANES):
            cut = slice(p * LANES, (p + 1) * LANES)
            masked = jnp.where(col_ids < row_ids[:, cut], scores[:, cut], EMPTY)
            parts.append(jnp.max(masked, axis=0, keepdims=True))
        acc[row, :, row_at] = jnp.maximum(acc[row, :, row_at], jnp.concatenate(parts, axis=1))

    whole = pl.ds(0, rows)

    acc[0] = prior[...]
    for s in range(1, 2 + slots):
        acc[s] = jnp.full((1, rows), EMPTY, jnp.float32)
    idv[0] = ids[...]
    local.wait()

    @pl.loop(0, CHUNKS)
    def _(c):
        ready(0, c)

    me = g * n_blk + b

    def to_device(step):
        other = (me + step) % devices
        return other, other // n_blk, other % n_blk

    @pl.loop(1, devices)
    def _(step):
        other, og, ob = to_device(step)
        remote(obuf.at[other], rows_out.at[me], rows_send, rows_recv, ob, og).start()
        remote(oid.at[other], ids_out.at[me], oids_send, oids_recv, ob, og).start()

    keep_rows = pltpu.make_async_copy(obuf.at[me], rows_out.at[me], keep_sem.at[0])
    keep_ids = pltpu.make_async_copy(oid.at[me], ids_out.at[me], keep_sem.at[1])
    keep_rows.start()
    keep_ids.start()

    def is_row(u, v):
        diff = (u - v + n_blk) % n_blk
        return (diff >= 1) & (diff <= CYCLE)

    def against_whole(s, c, other):
        @pl.when(is_row(blocks[s], blocks[other]))
        def _():
            tile(s, span(c), ch, other, whole)

        @pl.when(is_row(blocks[other], blocks[s]))
        def _():
            tile(other, whole, rows, s, span(c))

    def against_part(s, c, other, count):
        @pl.when(is_row(blocks[s], blocks[other]))
        def _():
            @pl.loop(0, count)
            def _(j):
                tile(s, span(c), ch, other, span(j))

        @pl.when(is_row(blocks[other], blocks[s]))
        def _():
            @pl.loop(0, count)
            def _(j):
                tile(other, span(j), ch, s, span(c))

    def arrive(s, c):
        chunk_copy(raw.at[s, span(c), :], 0, s, partner, c).wait_recv()

        @pl.when(c == 0)
        def _():
            ids_copy(idv.at[s], 0, s, partner).wait_recv()

        if s >= 2:
            @pl.when(fwd_z[s - 2] >= 0)
            def _():
                forward_copy(s - 2, c).start()

                @pl.when(c == 0)
                def _():
                    ids_copy(idv.at[s], s, 2 + fwd_slot[s - 2], block_of(fwd_z[s - 2])).start()

    @pl.loop(0, CHUNKS)
    def _(c):
        tile(0, whole, rows, 0, span(c))

    @pl.loop(0, CHUNKS)
    def _(c):
        @pl.when(exists[0] == 1)
        def _():
            arrive(2, c)
            ready(2, c)
            against_whole(2, c, 0)

    @pl.when((own_z >= 0) & (is_late == 1))
    def _():
        start_own_column()

    @pl.loop(0, CHUNKS)
    def _(c):
        for s in range(1, slots):
            @pl.when(exists[s] == 1)
            def _(s=s):
                arrive(2 + s, c)
                ready(2 + s, c)
                against_whole(2 + s, c, 0)
                against_part(2 + s, c, 1, c)

        arrive(1, c)
        ready(1, c)

        @pl.when(is_row(b, partner))
        def _():
            tile(0, whole, rows, 1, span(c))

        @pl.when(exists[0] == 1)
        def _():
            against_whole(1, c, 2)

        for s in range(1, slots):
            @pl.when(exists[s] == 1)
            def _(s=s):
                against_part(1, c, 2 + s, c + 1)

    back = remote(acc.at[1], ret.at[0], ret_send.at[0], ret_recv.at[0], partner)
    back.start()
    for s in range(slots):
        @pl.when(exists[s] == 1)
        def _(s=s):
            remote(acc.at[2 + s], ret.at[1 + ranks[s]], ret_send.at[1 + s], ret_recv.at[1 + ranks[s]],
                   block_of(slot_z[s])).start()

    for c in range(CHUNKS):
        partner_copy(c).wait_send()
    ids_copy(ids, 0, 1, partner).wait_send()

    @pl.when(own_z >= 0)
    def _():
        for c in range(CHUNKS):
            own_column(c).wait_send()
        ids_copy(ids, 1, 2 + own_slot, block_of(own_z)).wait_send()

    for s in range(slots):
        @pl.when(fwd_z[s] >= 0)
        def _(s=s):
            for c in range(CHUNKS):
                forward_copy(s, c).wait_send()
            ids_copy(idv.at[2 + s], 2 + s, 2 + fwd_slot[s], block_of(fwd_z[s])).wait_send()

    keep_rows.wait()
    keep_ids.wait()
    others = pl.ds(0, devices - 1)
    pltpu.make_async_copy(obuf.at[others], rows_out.at[others], rows_send).wait()
    pltpu.make_async_copy(oid.at[others], ids_out.at[others], oids_send).wait()
    pltpu.make_async_copy(obuf.at[others], rows_out.at[others], rows_recv).wait()
    pltpu.make_async_copy(oid.at[others], ids_out.at[others], oids_recv).wait()

    back.wait_recv()
    run_out[...] = jnp.maximum(acc[0], ret[0])
    for k in range(max(returns)):
        @pl.when(k < n_returns)
        def _(k=k):
            remote(acc.at[1], ret.at[1 + k], ret_send.at[0], ret_recv.at[1 + k], partner).wait_recv()
            run_out[...] = jnp.maximum(run_out[...], ret[1 + k])

    back.wait_send()
    for s in range(slots):
        @pl.when(exists[s] == 1)
        def _(s=s):
            remote(acc.at[2 + s], ret.at[1 + ranks[s]], ret_send.at[1 + s], ret_recv.at[1 + ranks[s]],
                   block_of(slot_z[s])).wait_send()


def body(embeds, doc_ids, prior_max, owned, owned_ids, owner_dest):
    n_grp, n_blk = lax.axis_size("grp"), lax.axis_size("blk")
    devices = n_grp * n_blk
    plan = make_plan(n_blk // 2)
    received, returns = plan[0], plan[5]
    slots = max(len(entry) for entry in received)
    rows, width = embeds.shape[1:]
    own_dev = owned.shape[0]
    vmem = pl.BlockSpec(memory_space=pltpu.VMEM)
    anywhere = pl.BlockSpec(memory_space=pl.ANY)
    dma = pltpu.SemaphoreType.DMA
    running, next_rows, next_ids = pl.pallas_call(
        functools.partial(kernel, plan, (n_grp, n_blk)),
        out_shape=(
            jax.ShapeDtypeStruct((1, rows), jnp.float32),
            jax.ShapeDtypeStruct((devices, CAP, width), jnp.bfloat16),
            jax.ShapeDtypeStruct((devices, 1, LANES), jnp.int32),
        ),
        in_specs=[anywhere, vmem, vmem, vmem, vmem, vmem],
        out_specs=(vmem, anywhere, anywhere),
        scratch_shapes=[
            pltpu.VMEM((2 + slots, rows, width), jnp.bfloat16),
            pltpu.VMEM((2 + slots, rows, width), jnp.bfloat16),
            pltpu.VMEM((2 + slots, 1, rows), jnp.int32),
            pltpu.VMEM((2 + slots, rows, LANES), jnp.float32),
            pltpu.VMEM((2 + slots, 1, rows), jnp.float32),
            pltpu.VMEM((1 + max(returns), 1, rows), jnp.float32),
            pltpu.VMEM((devices, CAP, width), jnp.bfloat16),
            pltpu.VMEM((devices, 1, LANES), jnp.int32),
            dma, dma((2 + slots, CHUNKS)), dma((2 + slots, CHUNKS)),
            dma((2 + slots,)), dma((2 + slots,)),
            dma((1 + slots,)), dma((1 + max(returns),)),
            dma, dma, dma, dma, dma((2,)),
        ],
        compiler_params=pltpu.CompilerParams(has_side_effects=True, vmem_limit_bytes=60 * 1024 * 1024),
    )(embeds, doc_ids, prior_max, owned, owned_ids.reshape(1, own_dev), owner_dest)
    return (running, next_rows.reshape(devices * CAP, width), next_ids[:, 0, :CAP].reshape(devices * CAP))


def solution(mesh):
    return jax.shard_map(
        body,
        mesh=mesh,
        in_specs=(
            P("grp", "blk", None),
            P("grp", "blk"),
            P("grp", "blk"),
            P(("grp", "blk"), None),
            P(("grp", "blk")),
            P(("grp", "blk"), None),
        ),
        out_specs=(P("grp", "blk"), P(("grp", "blk"), None), P(("grp", "blk"))),
        check_vma=False,
    )
```

time: 184 us -> 95.7 us (0.52)
  waiting for transfers between devices: 140 us -> 0 us
  Pallas kernels: 0 us -> 89 us
  starting transfers between devices: 16 us -> 0 us
  matrix products: 15.6 us -> 0 us
  other arithmetic: 5.43 us -> 0 us
    ppermute x6 -> x0, waiting for transfers between devices: 97.1 us -> none  [passed_along(): return lax.ppermute(value, axis, pairs)]
    pallas_call x0 -> x1, Pallas kernels: none -> 89 us  [body(): pl.pallas_call(functools.partial(kernel, plan, (n_grp, n_blk)), out_shape...]
    all_to_all x2 -> x0, waiting for transfers between devices: 43 us -> none  [the longest x1 38.5 us: body(): lax.all_to_all(outgoing_ids.reshape(devices, CAP), ('grp', 'blk'), split_...]
    dot_general x4 -> x0, matrix products: 15.6 us -> none  [tile_max(): lax.dot_general(row_normed, col_normed, (((1,), (1,)), ((), ())), preferr...]
    all_to_all x2 -> x0, starting transfers between devices: 8.43 us -> none  [the longest x1 5.85 us: body(): lax.all_to_all(outgoing_ids.reshape(devices, CAP), ('grp', 'blk'), split_...]
    ppermute x6 -> x0, starting transfers between devices: 7.52 us -> none  [passed_along(): return lax.ppermute(value, axis, pairs)]
    reduce_sum x3 -> x0, other arithmetic: 2.52 us -> none  [the longest x2 2.34 us: normalize(): scale = lax.rsqrt(jnp.sum(values * values, axis=-1, keepdims=True) + 1e-06)]
  transfers between devices with their start and end apart: 8 -> 0, of which waited for: 4 -> 0; matrix products, arithmetic and copies ran while one was open for 9% -> 0% of each run, Pallas kernels for 0% -> 0%
where the time goes in v1:
time: 95.7 us; the launch traced here: 95.4 us
  Pallas kernels  89 us (93%)
  local copies, waits for them, and re-layouts  5.73 us (6%)
    pallas_call x1, Pallas kernels, body(): pl.pallas_call(functools.partial(kernel, plan, (n_grp, n_blk)), out_shape...  89 us
    unnamed x2, local copies, waits for them, and re-layouts  2.64 us

profile of v1, /device:TPU:0, one launch (start us, length us, event | category | flops | bytes accessed | tf_op | source)
XLA Modules:
  0.0 95.4 jit_solution(1115419367403926545)
XLA Ops:
  0.6 1.4 %copy.10.dest = s32[64,1]{1,0:T(8,128)} copy(s32[64,1]{0,1:T(1,128)} %param.11) | data formatting | bytes 512 | tf_op args[5]
  2.0 89.0 %shard_map.85 = (f32[1,1024]{1,0:T(1,128)}, bf16[32,4,1024]{2,1,0:T(4,128)(2,1)}, s32[32,1,128]{2,1,0:T(1,128)}) custom-call(bf16[1,1024,1024]{2,1,0:T(8,128)(2,1)} %emb.1, s32[1,1024]{1,0:T(1,128)} %ids.1, f32[1,1024]{1,0:T(1,128)} %prior.1, bf16[64,1024]{1,0:T(8,128)(2,1)} %owned.1, s32[1,64]{1,0:T(1,128)} %bitcast.1, s32[64,1]{1,0:T(8,128)} %copy.10.dest), custom_call_target="tpu_custom_call" | custom-call | tf_op jit(solution)/shard_map/pallas_call | solution.py:352
  91.0 0.8 slice_reduce_fusion
  91.8 0.6 reshape_squeeze.3
  92.4 1.7 %reshape.13 = bf16[128,1024]{1,0:T(8,128)(2,1)} reshape(bf16[32,4,1024]{2,1,0:T(4,128)(2,1)} %get-tuple-element.7) | data formatting | bytes 524288 | tf_op jit(solution)/shard_map/reshape | solution.py:377
  94.1 1.3 %copy.12 = f32[1,1024]{1,0:T(1,128)} copy(f32[1,1024]{1,0:T(1,128)} %get-tuple-element.12) | data formatting | bytes 8192
